TPU v7x, 32 devices: a whole 2x2x4 slice. The times are simulated.
32 devices in a mesh: wave: 16 (over z, x, core), lev: 2 (over y).
Axes of the slice: x: 2, y: 2, z: 4, core: 2. Of those that a mesh axis runs over, the one named last changes fastest.
Arguments:
- spectral: float32 [136, 256, 2562], P('lev', 'wave'), may hold values from -6 to 6
- to_modes: float32 [136, 136], replicated, may hold values from -3 to 3
- from_modes: float32 [136, 136], replicated, may hold values from -3 to 3
- depth: float32 [136], replicated, may hold values from 0.02 to 50
- owner: int32 [128], replicated, may hold values from 0 to 15, as said below
Outputs:
- solved: float32 [136, 128, 2562], P('lev', 'wave')
Inputs may be any that keep to these rules, and one draw needn't show every extreme that they name: `owner`: group q holds the pairs q * 1 to q * 1 + 1 - 1; a device stores its groups in increasing q from its first slot on, 1 slots each, and leaves its other slots unused. The 8 groups with the same q // 8 have 8 different owners. A device owns at most 16 groups, and some device exactly that many.
All inputs are finite; a program needn't handle non-finite values.
Results may differ from a plain program's by a relative error of at most 0.000075.
Values sent between devices are 32-bit elements; how exact they have to be, the bound alone decides.
A program may use at most 128 MiB of HBM per device.

v0:
```python
import functools

import jax
import jax.numpy as jnp
from jax import lax
from jax.experimental import pallas as pl
from jax.experimental.pallas import tpu as pltpu
from jax.sharding import PartitionSpec as P

NT = 1279
KPAIR = 1
LANES = 128
TILES = 3
AHEAD = 2
MESH = pl.DeviceIdType.MESH


def flipped(index, mask, count):
    result = index * 0
    bit = 1
    while bit < count:
        own = lax.rem(lax.div(index, bit), 2)
        result = result + bit * ((1 - own) if mask & bit else own)
        bit *= 2
    return result


def halves(value):
    high = value.astype(jnp.bfloat16)
    low = (value - high.astype(jnp.float32)).astype(jnp.bfloat16)
    return high, low


def product(left_both, left_high, right, rows):
    high, low = halves(right)
    both = jnp.dot(left_both, high, preferred_element_type=jnp.float32)
    cross = jnp.dot(left_high, low, preferred_element_type=jnp.float32)
    return (both[rows:] + cross) + both[:rows]


def kernel(sizes, picks, places, spectral, last, to_modes, from_modes, depth, solved, *scratch):
    waves, levs, pairs, slots, levels, width, parts, packs, rest = sizes
    chunks = len(parts)
    received, rows_in, sending, mine, theirs, staged = (
        scratch[kind * chunks : (kind + 1) * chunks] for kind in range(6)
    )
    rows_last, tail_sent, tail_got, tail_mine, tail_theirs = scratch[6 * chunks : 6 * chunks + 5]
    to_both, from_both, load_sem, send_sem, recv_sem, lev_send, lev_recv, out_sem = scratch[
        6 * chunks + 5 :
    ]
    me = lax.axis_index("wave")
    lev = lax.axis_index("lev")
    modes_number = depth.shape[0]
    firsts = [sum(parts[:c]) for c in range(chunks)]
    final = chunks - 1

    def load(c, tile):
        number = firsts[c] + tile
        if number < sum(parts):
            source = spectral.at[:, pl.ds(number * LANES, LANES)]
            return pltpu.make_async_copy(source, rows_in[c].at[tile], load_sem.at[number])
        target = rows_last.at[pl.ds(0, levels * slots)]
        return pltpu.make_async_copy(last, target, load_sem.at[number])

    def width_of(c):
        return parts[c] + (1 if c == final else 0)

    for c in range(chunks):
        for tile in range(width_of(c)):
            load(c, tile).start()

    barrier = pltpu.get_barrier_semaphore()
    for mask in range(1, waves):
        pl.semaphore_signal(
            barrier, inc=1, device_id={"wave": flipped(me, mask, waves)}, device_id_type=MESH
        )
    for turn in range(1, levs):
        pl.semaphore_signal(
            barrier, inc=1, device_id={"lev": lax.rem(lev + turn, levs)}, device_id_type=MESH
        )

    for part in range(levs):
        high, low = halves(to_modes[part])
        to_both[part, :modes_number] = high
        to_both[part, modes_number:] = low
    high, low = halves(from_modes[...])
    from_both[0], from_both[1] = high, low
    pl.semaphore_wait(barrier, waves + levs - 2)

    def packed(slot):
        lane = lax.broadcasted_iota(jnp.int32, (8, LANES), 1)
        total = rows_last[pl.ds(slot, 8, stride=slots), :]
        for k in range(1, packs):
            block = rows_last[pl.ds(8 * k * slots + slot, 8, stride=slots), :]
            total = jnp.where(lane >= k * rest, pltpu.roll(block, k * rest, 1), total)
        return total

    def unpacked(block):
        pieces = [block] + [pltpu.roll(block, LANES - k * rest, 1) for k in range(1, packs)]
        return jnp.concatenate(pieces, axis=0)[:levels]

    def send(c):
        for tile in range(width_of(c)):
            load(c, tile).wait()

        def pick(mask, target):
            slot = picks[flipped(me, mask, waves)]
            for tile in range(parts[c]):
                target[:, pl.ds(tile * LANES, LANES)] = rows_in[c][
                    tile, pl.ds(slot, levels, stride=slots), :
                ]

        def push(mask, source, target, number):
            pltpu.make_async_remote_copy(
                src_ref=source.at[mask - 1],
                dst_ref=target.at[mask],
                send_sem=send_sem.at[number],
                recv_sem=recv_sem.at[number],
                device_id={"wave": flipped(me, mask, waves)},
                device_id_type=MESH,
            ).start()

        if c == final:
            for mask in range(waves - 1, 0, -1):
                tail_sent[mask - 1] = packed(picks[flipped(me, mask, waves)])
                push(mask, tail_sent, tail_got, chunks)
            tail_got[0] = packed(picks[me])
        for mask in range(waves - 1, 0, -1):
            pick(mask, sending[c].at[mask - 1])
            push(mask, sending[c], received[c], c)
        pick(0, received[c].at[0])

    def lev_copy(c, turn):
        source, target = (tail_mine, tail_theirs) if c == chunks else (mine[c], theirs[c])
        return pltpu.make_async_remote_copy(
            src_ref=source,
            dst_ref=target.at[turn - 1],
            send_sem=lev_send.at[c, turn - 1],
            recv_sem=lev_recv.at[c, turn - 1],
            device_id={"lev": lax.rem(lev + turn, levs)},
            device_id_type=MESH,
        )

    def out_copy(c, tile):
        number = firsts[c] + tile
        columns = solved.at[:, pl.ds(number * LANES, LANES)]
        return pltpu.make_async_copy(staged[c].at[tile], columns, out_sem.at[number])

    def gather(c):
        if c == final:
            arrived = tail_got.at[pl.ds(1, waves - 1)]
            pltpu.make_async_copy(arrived, arrived, recv_sem.at[chunks]).wait()
            for pair in range(pairs):
                tail_mine[pair] = tail_got[places[pair]]
            for turn in range(1, levs):
                lev_copy(chunks, turn).start()
        arrived = received[c].at[pl.ds(1, waves - 1)]
        pltpu.make_async_copy(arrived, arrived, recv_sem.at[c]).wait()

        @pl.loop(0, pairs)
        def _(pair):
            mine[c][pair] = received[c][places[pair]]

        for turn in range(1, levs):
            lev_copy(c, turn).start()

    def solve(c):
        for turn in range(1, levs):
            lev_copy(c, turn).wait_recv()
            if c == final:
                lev_copy(chunks, turn).wait_recv()
        size = width_of(c) * LANES
        column = lax.broadcasted_iota(jnp.int32, (1, size), 1) + firsts[c] * LANES
        within = jnp.where(column >= width // 2, column - width // 2, column)

        @pl.loop(0, pairs)
        def _(pair):
            wavenumber = me * pairs + pair
            degree = jnp.where(within <= NT - wavenumber, wavenumber + within, within - 1)
            ratio = (degree * (degree + 1)).astype(jnp.float32) / float(NT * (NT + 1))
            modes = None
            for turn in range(levs):
                source = lax.rem(lev + levs - turn, levs)
                block = mine[c][pair] if turn == 0 else theirs[c][turn - 1, pair]
                if c == final:
                    tail = tail_mine[pair] if turn == 0 else tail_theirs[turn - 1, pair]
                    block = jnp.concatenate([block, unpacked(tail)], axis=1)
                matrix = to_both.at[source]
                term = product(matrix[...], matrix[:modes_number], block, modes_number)
                modes = term if modes is None else modes + term
            scaled = modes / (1.0 + depth[...] * ratio)
            high, low = halves(scaled)
            from_high = from_both[0]
            result = jnp.dot(from_both[1], high, preferred_element_type=jnp.float32)
            result += jnp.dot(from_high, low, preferred_element_type=jnp.float32)
            result += jnp.dot(from_high, high, preferred_element_type=jnp.float32)
            for tile in range(width_of(c)):
                staged[c][tile, pl.ds(pair, levels, stride=pairs), :] = result[
                    :, tile * LANES : (tile + 1) * LANES
                ]

        for tile in range(width_of(c)):
            out_copy(c, tile).start()

    for c in range(min(AHEAD, chunks)):
        send(c)
    for c in range(chunks):
        if c + AHEAD < chunks:
            send(c + AHEAD)
        gather(c)
        if c >= 1:
            solve(c - 1)
    solve(final)
    for c in range(chunks + 1):
        sent = tail_sent if c == chunks else sending[c]
        pltpu.make_async_copy(sent, sent, send_sem.at[c]).wait()
        for turn in range(1, levs):
            lev_copy(c, turn).wait_send()
    for c in range(chunks):
        for tile in range(width_of(c)):
            out_copy(c, tile).wait()


def per_device(spectral, to_modes, from_modes, depth, owner):
    waves, levs = lax.axis_size("wave"), lax.axis_size("lev")
    levels, slots, width = spectral.shape
    groups = owner.shape[0] // waves
    pairs = groups * KPAIR
    modes_number = depth.shape[0]
    own_index, lev_index = lax.axis_index("wave"), lax.axis_index("lev")
    numbers = jnp.arange(owner.shape[0], dtype=jnp.int32)
    mine = owner == own_index
    before = (numbers[:, None] > numbers[None, :]) & mine[None, :]
    rank = jnp.sum(before.astype(jnp.int32), axis=1)
    picks = jnp.sum(jnp.where(mine, rank, 0).reshape(waves, groups), axis=1)
    places = lax.dynamic_slice_in_dim(owner, own_index * groups, groups) ^ own_index
    whole, rest = width // LANES, width % LANES
    packs = pl.cdiv(levels, 8)
    assert 0 < rest and packs * rest <= LANES
    parts = (TILES,) * (whole // TILES) + ((whole % TILES,) if whole % TILES else ())
    chunks = len(parts)
    sizes = (waves, levs, pairs, slots, levels, width, parts, packs, rest)
    rows = spectral.reshape(levels * slots, width)
    last = jnp.pad(rows[:, whole * LANES :], ((0, 0), (0, LANES - rest)))
    by_lev = to_modes.reshape(modes_number, levs, levels).transpose(1, 0, 2)
    own_rows = lax.dynamic_slice_in_dim(from_modes, lev_index * levels, levels)
    vmem, smem, anywhere = (
        pl.BlockSpec(memory_space=space) for space in (pltpu.VMEM, pltpu.SMEM, pl.ANY)
    )
    dma = pltpu.SemaphoreType.DMA
    f32, bf16 = jnp.float32, jnp.bfloat16
    widths = [tiles * LANES for tiles in parts]
    staged_tiles = parts[:-1] + (parts[-1] + 1,)
    solved = pl.pallas_call(
        functools.partial(kernel, sizes),
        out_shape=jax.ShapeDtypeStruct((levels * pairs, (whole + 1) * LANES), f32),
        in_specs=[smem, smem, anywhere, anywhere, vmem, vmem, vmem],
        out_specs=anywhere,
        scratch_shapes=[pltpu.VMEM((waves, levels, size), f32) for size in widths]
        + [pltpu.VMEM((tiles, levels * slots, LANES), f32) for tiles in parts]
        + [pltpu.VMEM((waves - 1, levels, size), f32) for size in widths]
        + [pltpu.VMEM((pairs, levels, size), f32) for size in widths]
        + [pltpu.VMEM((levs - 1, pairs, levels, size), f32) for size in widths]
        + [pltpu.VMEM((tiles, levels * pairs, LANES), f32) for tiles in staged_tiles]
        + [
            pltpu.VMEM((8 * packs * slots, LANES), f32),
            pltpu.VMEM((waves - 1, 8, LANES), f32),
            pltpu.VMEM((waves, 8, LANES), f32),
            pltpu.VMEM((pairs, 8, LANES), f32),
            pltpu.VMEM((levs - 1, pairs, 8, LANES), f32),
            pltpu.VMEM((levs, 2 * modes_number, levels), bf16),
            pltpu.VMEM((2, levels, modes_number), bf16),
            dma((whole + 1,)),
            dma((chunks + 1,)),
            dma((chunks + 1,)),
            dma((chunks + 1, levs - 1)),
            dma((chunks + 1, levs - 1)),
            dma((whole + 1,)),
        ],
        compiler_params=pltpu.CompilerParams(
            collective_id=0, has_side_effects=True, vmem_limit_bytes=67043328
        ),
    )(picks, places, rows, last, by_lev, own_rows, depth[:, None])
    return solved.reshape(levels, pairs, (whole + 1) * LANES)[:, :, :width]


def solution(mesh):
    placed = (P("lev", "wave", None), P(), P(), P(), P())
    return jax.shard_map(
        per_device, mesh=mesh, in_specs=placed, out_specs=P("lev", "wave", None), check_vma=False
    )
```

profile of v0, /device:TPU:0, one launch (start us, length us, event | category | flops | bytes accessed | tf_op | source)
XLA Modules:
  0.0 311.9 jit_solution(14589652580087139613)
XLA Ops:
  0.0 1.3 dynamic-slice_xor_fusion.places
  1.3 0.7 broadcast_compare_fusion
  1.9 0.1 convert_reduce_fusion
  2.0 0.7 broadcast_select_fusion
  2.7 0.1 reshape.13
  2.8 0.6 reduce_sum.19.picks
  3.4 1.4 copy.11.depth
  4.8 1.5 constant_dynamic-slice_fusion.from_modes
  6.4 1.0 reshape.17
  7.4 0.7 copy.15
  8.1 1.1 slice.8
  9.2 0.8 pad.4.last
  10.0 296.3 %shard_map.55 = f32[544,2688]{1,0:T(8,128)} custom-call(s32[16]{0:T(128)} %reduce_sum.19.picks, s32[8]{0:T(128)} %dynamic-slice_xor_fusion.places, f32[1088,2562]{1,0:T(8,128)} %bitcast.9, f32[1088,128]{1,0:T(8,128)} %pad.4.last, f32[2,136,68]{2,1,0:T(8,128)} %bitcast.10, f32[68,136]{1,0:T(8,128)} %constant_dynamic-slice_fusion.from_modes, f32[136,1]{1,0:T(8,128)} %copy.11.depth), custom_call_target="tpu_custom_call" | custom-call | tf_op jit(solution)/shard_map/pallas_call | solution.py:254
  306.3 5.6 %copy.17 = f32[68,8,2562]{2,1,0:T(8,128)} copy(f32[68,8,2562]{2,1,0:T(8,128)} %bitcast.7) | data formatting | bytes 11149824
where the time goes:
time: 312 us
  Pallas kernels  296 us (95%)
  local copies, waits for them, and re-layouts  12.3 us (4%)
  other arithmetic  3.32 us (1%)
    pallas_call x1, Pallas kernels, per_device(): pl.pallas_call(functools.partial(kernel, sizes), out_shape=jax.ShapeDtype...  296 us

commit v1 on v0

--- a/solution.py
+++ b/solution.py
@@ -11,8 +11,18 @@
 KPAIR = 1
 LANES = 128
 TILES = 3
+HEAD = (1, 2, 2)
+TAIL = (2, 2, 1, 1)
 AHEAD = 2
 MESH = pl.DeviceIdType.MESH
+
+
+def split(whole):
+    middle = whole - sum(HEAD) - sum(TAIL)
+    if middle < 0:
+        return (1,) * whole
+    rest = (middle % TILES,) if middle % TILES else ()
+    return HEAD + (TILES,) * (middle // TILES) + rest + TAIL
 
 
 def flipped(index, mask, count):
@@ -237,7 +247,7 @@
     whole, rest = width // LANES, width % LANES
     packs = pl.cdiv(levels, 8)
     assert 0 < rest and packs * rest <= LANES
-    parts = (TILES,) * (whole // TILES) + ((whole % TILES,) if whole % TILES else ())
+    parts = split(whole)
     chunks = len(parts)
     sizes = (waves, levs, pairs, slots, levels, width, parts, packs, rest)
     rows = spectral.reshape(levels * slots, width)

time: 312 us -> 301 us (0.965)
  Pallas kernels: 296 us -> 285 us
    pallas_call x1, Pallas kernels: 296 us -> 285 us  [per_device(): pl.pallas_call(functools.partial(kernel, sizes), out_shape=jax.ShapeDtype...]
where the time goes in v1:
time: 301 us
  Pallas kernels  285 us (95%)
  local copies, waits for them, and re-layouts  12.3 us (4%)
  other arithmetic  3.32 us (1%)
    pallas_call x1, Pallas kernels, per_device(): pl.pallas_call(functools.partial(kernel, sizes), out_shape=jax.ShapeDtype...  285 us

profile of v1, /device:TPU:0, one launch (start us, length us, event | category | flops | bytes accessed | tf_op | source)
XLA Modules:
  0.0 300.6 jit_solution(16570429923740240786)
XLA Ops:
  0.0 1.3 dynamic-slice_xor_fusion.places
  1.3 0.7 broadcast_compare_fusion
  1.9 0.1 convert_reduce_fusion
  2.0 0.7 broadcast_select_fusion
  2.7 0.1 reshape.13
  2.8 0.6 reduce_sum.19.picks
  3.4 1.4 copy.11.depth
  4.8 1.5 constant_dynamic-slice_fusion.from_modes
  6.4 1.0 reshape.17
  7.4 0.7 copy.15
  8.1 1.1 slice.8
  9.2 0.8 pad.4.last
  10.0 284.9 %shard_map.55 = f32[544,2688]{1,0:T(8,128)} custom-call(s32[16]{0:T(128)} %reduce_sum.19.picks, s32[8]{0:T(128)} %dynamic-slice_xor_fusion.places, f32[1088,2562]{1,0:T(8,128)} %bitcast.9, f32[1088,128]{1,0:T(8,128)} %pad.4.last, f32[2,136,68]{2,1,0:T(8,128)} %bitcast.10, f32[68,136]{1,0:T(8,128)} %constant_dynamic-slice_fusion.from_modes, f32[136,1]{1,0:T(8,128)} %copy.11.depth), custom_call_target="tpu_custom_call" | custom-call | tf_op jit(solution)/shard_map/pallas_call | solution.py:264
  295.0 5.6 %copy.17 = f32[68,8,2562]{2,1,0:T(8,128)} copy(f32[68,8,2562]{2,1,0:T(8,128)} %bitcast.7) | data formatting | bytes 11149824

commit v2 on v1

--- a/solution.py
+++ b/solution.py
@@ -14,6 +14,9 @@
 HEAD = (1, 2, 2)
 TAIL = (2, 2, 1, 1)
 AHEAD = 2
+QUAD = 4
+RING = 3
+LAGS = (0, 1, 2, 3, 4)
 MESH = pl.DeviceIdType.MESH
 
 
@@ -229,6 +232,409 @@
     for c in range(chunks):
         for tile in range(width_of(c)):
             out_copy(c, tile).wait()
+
+
+def relay_kernel(sizes, picks, places, relayed, landed, spectral, last, to_modes, from_modes, depth, solved, *scratch):
+    waves, levs, pairs, slots, levels, width, parts, packs, rest, room = sizes
+    chunks = len(parts)
+    scratch = list(scratch)
+
+    def take(count):
+        taken = scratch[:count]
+        del scratch[:count]
+        return taken
+
+    received, carried, arrived_far, final_far, theirs = (take(chunks) for _ in range(5))
+    rows_in, direct_out, carry_out, relay_out, forward_out, mine, staged = (
+        take(RING) for _ in range(7)
+    )
+    rows_last, tail_sent, tail_got, tail_mine, tail_theirs, to_both, from_both = take(7)
+    (load_sem, direct_send, direct_recv, carry_send, carry_recv, relay_send, relay_recv,
+     forward_send, forward_recv, lev_send, lev_recv, out_sem) = take(12)
+    me = lax.axis_index("wave")
+    lev = lax.axis_index("lev")
+    half = waves // 2
+    side = lax.div(me, half)
+    step = lax.rem(lax.div(me, QUAD), 2)
+    quad = lax.rem(me, QUAD)
+    core = lax.rem(me, 2)
+    outer = lax.rem(side + step + 1, 2)
+    cut = levels // 2 // 8 * 8
+    part_rows = levels - cut
+    modes_number = depth.shape[0]
+    firsts = [sum(parts[:c]) for c in range(chunks)]
+    final = chunks - 1
+
+    def ring(buffers, c):
+        ref = buffers[c % RING]
+        size = parts[c] * LANES
+        if ref.shape[-1] == size:
+            return ref
+        return ref.at[tuple(slice(None) for _ in ref.shape[:-1]) + (pl.ds(0, size),)]
+
+    def to_wave(index):
+        return {"wave": index}
+
+    def load(c, tile):
+        number = firsts[c] + tile
+        if tile < parts[c]:
+            source = spectral.at[:, pl.ds(number * LANES, LANES)]
+            return pltpu.make_async_copy(source, rows_in[c % RING].at[tile], load_sem.at[number])
+        target = rows_last.at[pl.ds(0, levels * slots)]
+        return pltpu.make_async_copy(last, target, load_sem.at[number])
+
+    def width_of(c):
+        return parts[c] + (1 if c == final else 0)
+
+    def finish(ref, semaphore):
+        pltpu.make_async_copy(ref, ref, semaphore).wait()
+
+    def push(source, target, send_sem, recv_sem, index):
+        pltpu.make_async_remote_copy(
+            src_ref=source,
+            dst_ref=target,
+            send_sem=send_sem,
+            recv_sem=recv_sem,
+            device_id=to_wave(index),
+            device_id_type=MESH,
+        ).start()
+
+    load(final, parts[final]).start()
+    for c in range(min(RING, chunks)):
+        for tile in range(parts[c]):
+            load(c, tile).start()
+
+    barrier = pltpu.get_barrier_semaphore()
+    for mask in range(1, waves):
+        pl.semaphore_signal(
+            barrier, inc=1, device_id=to_wave(flipped(me, mask, waves)), device_id_type=MESH
+        )
+    for turn in range(1, levs):
+        pl.semaphore_signal(
+            barrier, inc=1, device_id={"lev": lax.rem(lev + turn, levs)}, device_id_type=MESH
+        )
+    for part in range(levs):
+        high, low = halves(to_modes[part])
+        to_both[part, :modes_number] = high
+        to_both[part, modes_number:] = low
+    high, low = halves(from_modes[...])
+    from_both[0], from_both[1] = high, low
+    pl.semaphore_wait(barrier, waves + levs - 2)
+
+    def packed(slot):
+        lane = lax.broadcasted_iota(jnp.int32, (8, LANES), 1)
+        total = rows_last[pl.ds(slot, 8, stride=slots), :]
+        for k in range(1, packs):
+            block = rows_last[pl.ds(8 * k * slots + slot, 8, stride=slots), :]
+            total = jnp.where(lane >= k * rest, pltpu.roll(block, k * rest, 1), total)
+        return total
+
+    def unpacked(block):
+        pieces = [block] + [pltpu.roll(block, LANES - k * rest, 1) for k in range(1, packs)]
+        return jnp.concatenate(pieces, axis=0)[:levels]
+
+    def drain_send(c):
+        finish(ring(direct_out, c), direct_send.at[c])
+        carry = ring(carry_out, c)
+
+        @pl.when(outer == 1)
+        def _():
+            finish(carry, carry_send.at[c])
+
+        @pl.when(outer == 0)
+        def _():
+            finish(carry.at[pl.ds(1, QUAD - 1)], carry_send.at[c])
+
+    def send(c):
+        for tile in range(width_of(c)):
+            load(c, tile).wait()
+        if c >= RING:
+            drain_send(c - RING)
+        source = rows_in[c % RING]
+        carry, direct = ring(carry_out, c), ring(direct_out, c)
+
+        def pick(slot, target, first, count):
+            for tile in range(parts[c]):
+                target[:, pl.ds(tile * LANES, LANES)] = source[
+                    tile, pl.ds(first * slots + slot, count, stride=slots), :
+                ]
+
+        for mask in range(QUAD - 1, -1, -1):
+            carrier = flipped(quad, mask, QUAD)
+            first = lax.rem(carrier, 2) * cut
+
+            @pl.loop(0, QUAD)
+            def _(j):
+                index = (1 - side) * half + lax.div(j, 2) * QUAD
+                index = index + lax.div(carrier, 2) * 2 + lax.rem(j, 2)
+                pick(picks[index], carry.at[mask, j], first, part_rows)
+
+            place = (mask + QUAD * outer) * QUAD
+            device = side * half + (1 - side) * QUAD + carrier
+
+            def carry_on():
+                target = carried[c].at[pl.ds(place, QUAD)]
+                push(carry.at[mask], target, carry_send.at[c], carry_recv.at[c], device)
+
+            if mask:
+                carry_on()
+            else:
+                pl.when(outer == 1)(carry_on)
+
+                @pl.when(outer == 0)
+                def _():
+                    @pl.loop(0, QUAD)
+                    def _(j):
+                        carried[c][j] = carry[0, j]
+
+        if c == final:
+            for mask in range(waves - 1, 0, -1):
+                index = flipped(me, mask, waves)
+                tail_sent[mask - 1] = packed(picks[index])
+                push(
+                    tail_sent.at[mask - 1],
+                    tail_got.at[mask],
+                    direct_send.at[chunks],
+                    direct_recv.at[chunks],
+                    index,
+                )
+            tail_got[0] = packed(picks[me])
+        for mask in range(half - 1, 0, -1):
+            index = flipped(me, mask, waves)
+            pick(picks[index], direct.at[mask - 1], 0, levels)
+            push(
+                direct.at[mask - 1],
+                received[c].at[mask],
+                direct_send.at[c],
+                direct_recv.at[c],
+                index,
+            )
+        pick(picks[me], received[c].at[0], 0, levels)
+        if c + RING < chunks:
+            for tile in range(parts[c + RING]):
+                load(c + RING, tile).start()
+
+    def relay(c):
+        @pl.when(outer == 0)
+        def _():
+            finish(carried[c].at[pl.ds(QUAD, (half - 1) * QUAD)], carry_recv.at[c])
+            if c >= RING:
+                finish(ring(relay_out, c - RING), relay_send.at[c - RING])
+            block = ring(relay_out, c)
+
+            @pl.loop(0, room)
+            def _(g):
+                block[g] = carried[c][relayed[g]]
+
+            push(
+                block, arrived_far[c], relay_send.at[c], relay_recv.at[c],
+                flipped(me, 3 * QUAD, waves),
+            )
+
+    def forward(c):
+        @pl.when(outer == 0)
+        def _():
+            finish(arrived_far[c], relay_recv.at[c])
+            if c >= RING:
+                finish(ring(forward_out, c - RING), forward_send.at[c - RING])
+            block = ring(forward_out, c)
+            for number, mask in enumerate((QUAD + 1, QUAD, 1)):
+
+                @pl.loop(0, pairs)
+                def _(pair):
+                    block[number, pair] = arrived_far[c][landed[number * pairs + pair]]
+
+                push(
+                    block.at[number],
+                    final_far[c].at[mask % 2],
+                    forward_send.at[c],
+                    forward_recv.at[c],
+                    flipped(me, mask, waves),
+                )
+
+            @pl.loop(0, pairs)
+            def _(pair):
+                final_far[c][0, pair] = arrived_far[c][landed[3 * pairs + pair]]
+
+    def lev_copy(c, turn):
+        source, target = (
+            (tail_mine, tail_theirs) if c == chunks else (ring(mine, c), theirs[c])
+        )
+        return pltpu.make_async_remote_copy(
+            src_ref=source,
+            dst_ref=target.at[turn - 1],
+            send_sem=lev_send.at[c, turn - 1],
+            recv_sem=lev_recv.at[c, turn - 1],
+            device_id={"lev": lax.rem(lev + turn, levs)},
+            device_id_type=MESH,
+        )
+
+    def out_copy(c, tile):
+        number = firsts[c] + tile
+        columns = solved.at[:, pl.ds(number * LANES, LANES)]
+        return pltpu.make_async_copy(staged[c % RING].at[tile], columns, out_sem.at[number])
+
+    def gather(c):
+        if c == final:
+            finish(tail_got.at[pl.ds(1, waves - 1)], direct_recv.at[chunks])
+            for pair in range(pairs):
+                tail_mine[pair] = tail_got[places[pair]]
+            for turn in range(1, levs):
+                lev_copy(chunks, turn).start()
+        finish(received[c].at[pl.ds(1, half - 1)], direct_recv.at[c])
+
+        @pl.when(outer == 1)
+        def _():
+            finish(final_far[c], forward_recv.at[c])
+
+        @pl.when(outer == 0)
+        def _():
+            finish(final_far[c].at[1], forward_recv.at[c])
+
+        if c >= RING:
+            for turn in range(1, levs):
+                lev_copy(c - RING, turn).wait_send()
+        block = ring(mine, c)
+
+        @pl.loop(0, pairs)
+        def _(pair):
+            place = places[pair]
+            far = place >= half
+            near = received[c][lax.rem(place, half)]
+            block[pair, pl.ds(0, cut)] = jnp.where(
+                far, final_far[c][core, pair, pl.ds(0, cut), :], near[:cut]
+            )
+            block[pair, pl.ds(cut, part_rows)] = jnp.where(
+                far, final_far[c][1 - core, pair], near[cut:]
+            )
+
+        for turn in range(1, levs):
+            lev_copy(c, turn).start()
+
+    def solve(c):
+        for turn in range(1, levs):
+            lev_copy(c, turn).wait_recv()
+            if c == final:
+                lev_copy(chunks, turn).wait_recv()
+        if c >= RING:
+            for tile in range(width_of(c - RING)):
+                out_copy(c - RING, tile).wait()
+        size = width_of(c) * LANES
+        column = lax.broadcasted_iota(jnp.int32, (1, size), 1) + firsts[c] * LANES
+        within = jnp.where(column >= width // 2, column - width // 2, column)
+        own, results = ring(mine, c), staged[c % RING]
+
+        @pl.loop(0, pairs)
+        def _(pair):
+            wavenumber = me * pairs + pair
+            degree = jnp.where(within <= NT - wavenumber, wavenumber + within, within - 1)
+            ratio = (degree * (degree + 1)).astype(jnp.float32) / float(NT * (NT + 1))
+            modes = None
+            for turn in range(levs):
+                source = lax.rem(lev + levs - turn, levs)
+                block = own[pair] if turn == 0 else theirs[c][turn - 1, pair]
+                if c == final:
+                    tail = tail_mine[pair] if turn == 0 else tail_theirs[turn - 1, pair]
+                    block = jnp.concatenate([block, unpacked(tail)], axis=1)
+                matrix = to_both.at[source]
+                term = product(matrix[...], matrix[:modes_number], block, modes_number)
+                modes = term if modes is None else modes + term
+            scaled = modes / (1.0 + depth[...] * ratio)
+            high, low = halves(scaled)
+            from_high = from_both[0]
+            result = jnp.dot(from_both[1], high, preferred_element_type=jnp.float32)
+            result += jnp.dot(from_high, low, preferred_element_type=jnp.float32)
+            result += jnp.dot(from_high, high, preferred_element_type=jnp.float32)
+            for tile in range(width_of(c)):
+                results[tile, pl.ds(pair, levels, stride=pairs), :] = result[
+                    :, tile * LANES : (tile + 1) * LANES
+                ]
+
+        for tile in range(width_of(c)):
+            out_copy(c, tile).start()
+
+    stages = (send, relay, forward, gather, solve)
+    for turn in range(chunks + LAGS[-1]):
+        for stage, lag in zip(stages, LAGS):
+            if 0 <= turn - lag < chunks:
+                stage(turn - lag)
+    finish(tail_sent, direct_send.at[chunks])
+    for turn in range(1, levs):
+        lev_copy(chunks, turn).wait_send()
+    for c in range(max(chunks - RING, 0), chunks):
+        drain_send(c)
+
+        @pl.when(outer == 0)
+        def _():
+            finish(ring(relay_out, c), relay_send.at[c])
+            finish(ring(forward_out, c), forward_send.at[c])
+
+        for turn in range(1, levs):
+            lev_copy(c, turn).wait_send()
+        for tile in range(width_of(c)):
+            out_copy(c, tile).wait()
+
+
+def relay_call(waves, levs, pairs, slots, levels, width, packs, rest, room, whole, modes_number):
+    parts = (1,) * whole
+    chunks = len(parts)
+    half = waves // 2
+    part_rows = levels - levels // 2 // 8 * 8
+    sizes = (waves, levs, pairs, slots, levels, width, parts, packs, rest, room)
+    widths = [tiles * LANES for tiles in parts]
+    most = [max(parts[c::RING]) for c in range(RING)]
+    ends = [max(parts[c] + (c == chunks - 1) for c in range(k, chunks, RING)) for k in range(RING)]
+    vmem, smem, anywhere = (
+        pl.BlockSpec(memory_space=space) for space in (pltpu.VMEM, pltpu.SMEM, pl.ANY)
+    )
+    dma = pltpu.SemaphoreType.DMA
+    f32, bf16 = jnp.float32, jnp.bfloat16
+
+    def vectors(*shape):
+        return pltpu.VMEM(shape, f32)
+
+    return pl.pallas_call(
+        functools.partial(relay_kernel, sizes),
+        out_shape=jax.ShapeDtypeStruct((levels * pairs, (whole + 1) * LANES), f32),
+        in_specs=[smem, smem, smem, smem, anywhere, anywhere, vmem, vmem, vmem],
+        out_specs=anywhere,
+        scratch_shapes=[vectors(half, levels, size) for size in widths]
+        + [vectors(half * QUAD, part_rows, size) for size in widths]
+        + [vectors(room, part_rows, size) for size in widths]
+        + [vectors(2, pairs, part_rows, size) for size in widths]
+        + [vectors(levs - 1, pairs, levels, size) for size in widths]
+        + [vectors(tiles, levels * slots, LANES) for tiles in most]
+        + [vectors(half - 1, levels, tiles * LANES) for tiles in most]
+        + [vectors(QUAD, QUAD, part_rows, tiles * LANES) for tiles in most]
+        + [vectors(room, part_rows, tiles * LANES) for tiles in most]
+        + [vectors(3, pairs, part_rows, tiles * LANES) for tiles in most]
+        + [vectors(pairs, levels, tiles * LANES) for tiles in most]
+        + [vectors(tiles, levels * pairs, LANES) for tiles in ends]
+        + [
+            vectors(8 * packs * slots, LANES),
+            vectors(waves - 1, 8, LANES),
+            vectors(waves, 8, LANES),
+            vectors(pairs, 8, LANES),
+            vectors(levs - 1, pairs, 8, LANES),
+            pltpu.VMEM((levs, 2 * modes_number, levels), bf16),
+            pltpu.VMEM((2, levels, modes_number), bf16),
+            dma((whole + 1,)),
+            dma((chunks + 1,)),
+            dma((chunks + 1,)),
+            dma((chunks,)),
+            dma((chunks,)),
+            dma((chunks,)),
+            dma((chunks,)),
+            dma((chunks,)),
+            dma((chunks,)),
+            dma((chunks + 1, levs - 1)),
+            dma((chunks + 1, levs - 1)),
+            dma((whole + 1,)),
+        ],
+        compiler_params=pltpu.CompilerParams(
+            collective_id=1, has_side_effects=True, vmem_limit_bytes=67043328
+        ),
+    )
 
 
 def per_device(spectral, to_modes, from_modes, depth, owner):
@@ -261,7 +667,7 @@
     f32, bf16 = jnp.float32, jnp.bfloat16
     widths = [tiles * LANES for tiles in parts]
     staged_tiles = parts[:-1] + (parts[-1] + 1,)
-    solved = pl.pallas_call(
+    dense = pl.pallas_call(
         functools.partial(kernel, sizes),
         out_shape=jax.ShapeDtypeStruct((levels * pairs, (whole + 1) * LANES), f32),
         in_specs=[smem, smem, anywhere, anywhere, vmem, vmem, vmem],
@@ -290,7 +696,33 @@
         compiler_params=pltpu.CompilerParams(
             collective_id=0, has_side_effects=True, vmem_limit_bytes=67043328
         ),
-    )(picks, places, rows, last, by_lev, own_rows, depth[:, None])
+    )
+    operands = (rows, last, by_lev, own_rows, depth[:, None])
+    if waves == 4 * QUAD:
+        half = waves // 2
+        room = half * QUAD * 3 // 4
+        owners = owner.reshape(2, 2, 2, 2, groups).transpose(0, 2, 1, 3, 4).reshape(2, 2, QUAD * groups)
+        crossing = (owners // half != jnp.arange(2)[:, None, None]).astype(jnp.int32)
+        inclusive = jnp.tril(jnp.ones((QUAD * groups,) * 2, jnp.int32))
+        before = jnp.sum(crossing[:, :, None, :] * inclusive, axis=-1)
+        fits = jnp.max(before[:, :, -1]) <= room
+        side, column = own_index // half, own_index // 2 % 2
+        there = before[1 - side, column] - 1
+        taken = (there[None, :] == jnp.arange(room)[:, None]) & (crossing[1 - side, column] > 0)[None, :]
+        target = jnp.arange(QUAD * groups, dtype=jnp.int32) // groups
+        number = ((owners[1 - side, column] ^ own_index) % half) * QUAD + target
+        relayed = jnp.sum(jnp.where(taken, number[None, :], 0), axis=1).astype(jnp.int32)
+        here = jnp.where(crossing[side, column] > 0, before[side, column] - 1, 0).reshape(QUAD, groups)
+        own_target = own_index // QUAD % 2 * 2 + own_index % 2
+        landed = here[own_target ^ jnp.array([3, 2, 1, 0])].reshape(-1).astype(jnp.int32)
+        solved = lax.cond(
+            fits,
+            lambda *given: relay_call(waves, levs, pairs, slots, levels, width, packs, rest, room, whole, modes_number)(*given),
+            lambda one, two, three, four, *given: dense(one, two, *given),
+            *(picks, places, relayed, landed, *operands),
+        )
+    else:
+        solved = dense(picks, places, *operands)
     return solved.reshape(levels, pairs, (whole + 1) * LANES)[:, :, :width]
 
 

time: 301 us -> 255 us (0.85)
  Pallas kernels: 285 us -> 228 us
  other arithmetic: 3.32 us -> 8.38 us
  local copies, waits for them, and re-layouts: 12.3 us -> 16.4 us
    pallas_call x1, Pallas kernels: 285 us -> 228 us  [per_device(): relay_call(waves, levs, pairs, slots, levels, width, packs, rest, room, w...]
    unnamed x1 -> x7, local copies, waits for them, and re-layouts: 5.59 us -> 6.19 us
where the time goes in v2:
time: 255 us; the launch traced here: 254 us
  Pallas kernels  228 us (89%)
  local copies, waits for them, and re-layouts  16.4 us (6%)
  other arithmetic  8.38 us (3%)
    pallas_call x1, Pallas kernels, per_device(): relay_call(waves, levs, pairs, slots, levels, width, packs, rest, room, w...  228 us
    unnamed x7, local copies, waits for them, and re-layouts  6.19 us

profile of v2, /device:TPU:0, one launch (start us, length us, event | category | flops | bytes accessed | tf_op | source)
XLA Modules:
  0.0 253.9 jit_solution(17168199566932736605)
XLA Ops:
  0.0 1.3 dynamic-slice_xor_fusion
  1.3 0.7 broadcast_compare_fusion
  2.0 0.1 convert_reduce_fusion
  2.1 0.7 broadcast_select_fusion
  2.7 0.5 iota.41
  3.3 0.1 reshape.145
  3.4 0.7 reduce_sum.43
  4.0 0.7 reshape.143
  4.8 0.1 reshape.144
  4.9 0.0 copy-start.2
  4.9 0.0 copy-start
  4.9 0.6 eq.40
  5.5 0.1 multiply_reduce_fusion
  5.6 0.0 copy-done
  5.7 0.0 copy-start.1
  5.7 0.6 copy-done.1
  6.2 0.7 slice_reduce_fusion
  7.6 1.5 constant_dynamic-slice_fusion.5
  9.1 0.0 copy-done.2
  9.2 1.0 reshape.159
  10.2 0.1 copy.25
  10.3 1.1 slice.26
  11.4 0.8 pad.4
  12.3 236.0 %conditional.1 = (f32[68,8,2562]{2,1,0:T(8,128)}) conditional(s32[]{:T(128)} %convert_element_type.16, (s32[16]{0:T(128)}, s32[8]{0:T(128)}, f32[1088,2562]{1,0:T(8,128)}, f32[1088,128]{1,0:T(8,128)}, f32[2,136,68]{1,2,0:T(8,128)S(1)}, /*index=5*/f32[68,136]{1,0:T(8,128)}, f32[136,1]{0,1:T(1,128)}) %tuple.90, (s32[2,2,32]{2,1,0:T(2,128)}, ...), branch_computations={%region_4.5_spmd, %region_5.7_spmd.clone.clone} | conditional | flops 4984 | bytes 158998 | solution.py:718
  12.3 0.7 compare_select_fusion
  13.0 0.7 fusion.9
  13.6 0.7 compare_bitcast_fusion
  14.3 0.7 fusion.8
  15.0 1.4 select_reduce_fusion.relayed
  16.4 0.1 select_n.161
  16.5 0.6 gather_fusion
  17.1 0.6 reshape.162.landed
  17.7 1.4 copy.27.depth
  19.1 0.8 copy.26.to_modes
  19.9 228.2 %branch_1_fun.5 = f32[544,2688]{1,0:T(8,128)} custom-call(s32[16]{0:T(128)} %get-tuple-element.724.picks, s32[8]{0:T(128)} %get-tuple-element.725.places, s32[24]{0:T(128)} %select_reduce_fusion.relayed, s32[32]{0:T(128)} %reshape.162.landed, f32[1088,2562]{1,0:T(8,128)} %get-tuple-element.726.spectral, f32[1088,128]{1,0:T(8,128)} %get-tuple-element.727.last, ...), custom_call_target="tpu_custom_call" | custom-call | tf_op jit(solution)/shard_map/cond/branch_1_fun/pallas_call | solution.py:720
  248.3 5.6 %copy.31 = f32[68,8,2562]{2,1,0:T(8,128)} copy(f32[68,8,2562]{2,1,0:T(8,128)} %get-tuple-element.575) | data formatting | bytes 11149824
  (4 shorter events, 0.0 us)
Async XLA Ops:
  4.9 4.3 %copy-start.2 = (s32[2,2,32]{2,1,0:T(2,128)}, s32[2,2,32]{2,1,0:T(2,128)S(1)}, u32[]{:S(2)}) copy-start(s32[2,2,32]{2,1,0:T(2,128)S(1)} %reshape.144) | copy-start | bytes 1540
  4.9 0.8 copy-start
  5.7 0.6 copy-start.1

commit v3 on v2

--- a/solution.py
+++ b/solution.py
@@ -15,6 +15,7 @@
 TAIL = (2, 2, 1, 1)
 AHEAD = 2
 QUAD = 4
+GROUP = 4
 RING = 3
 LAGS = (0, 1, 2, 3, 4)
 MESH = pl.DeviceIdType.MESH
@@ -42,6 +43,62 @@
     high = value.astype(jnp.bfloat16)
     low = (value - high.astype(jnp.float32)).astype(jnp.bfloat16)
     return high, low
+
+
+def upright(row):
+    count = row.shape[1]
+    across = lax.broadcasted_iota(jnp.int32, (count, count), 1)
+    down = lax.broadcasted_iota(jnp.int32, (count, count), 0)
+    return jnp.sum(jnp.where(across == down, row[...], 0.0), axis=1, keepdims=True)
+
+
+def tables(waves, groups, room, owner, picks, places, relayed, landed, fits, crossed):
+    half = waves // 2
+    me = lax.axis_index("wave")
+    side, column = lax.div(me, half), lax.rem(lax.div(me, 2), 2)
+    own_target = lax.rem(lax.div(me, QUAD), 2) * 2 + lax.rem(me, 2)
+    for target in range(waves):
+        picks[target] = 0
+    for slot in range(room):
+        relayed[slot] = 0
+    for pool in range(4):
+        crossed[pool] = 0
+
+    def per_target(target, rank):
+        there = lax.div(target, half)
+        pool = there * 2 + lax.rem(lax.div(target, 2), 2)
+        j = lax.rem(lax.div(target, QUAD), 2) * 2 + lax.rem(target, 2)
+        relays = pool == (1 - side) * 2 + column
+        lands = pool == side * 2 + column
+        number = (QUAD - 1 - (j ^ own_target)) * groups
+        position = crossed[pool]
+        for group in range(groups):
+            source = owner[target * groups + group]
+            mine = source == me
+            picks[target] = jnp.where(mine, rank, picks[target])
+            rank = rank + mine.astype(jnp.int32)
+            crossing = lax.div(source, half) != there
+            slot = jnp.minimum(position, room - 1)
+
+            @pl.when(relays & crossing)
+            def _():
+                relayed[slot] = lax.rem(source ^ me, half) * QUAD + j
+
+            @pl.when(lands)
+            def _():
+                landed[number + group] = jnp.where(crossing, slot, 0)
+
+            position = position + crossing.astype(jnp.int32)
+        crossed[pool] = position
+        return rank
+
+    lax.fori_loop(0, waves, per_target, jnp.int32(0))
+    for group in range(groups):
+        places[group] = owner[me * groups + group] ^ me
+    most = jnp.maximum(
+        jnp.maximum(crossed[0], crossed[1]), jnp.maximum(crossed[2], crossed[3])
+    )
+    fits[0] = (most <= room).astype(jnp.int32)
 
 
 def product(left_both, left_high, right, rows):
@@ -63,7 +120,7 @@
     ]
     me = lax.axis_index("wave")
     lev = lax.axis_index("lev")
-    modes_number = depth.shape[0]
+    modes_number = depth.shape[1]
     firsts = [sum(parts[:c]) for c in range(chunks)]
     final = chunks - 1
 
@@ -93,11 +150,16 @@
         )
 
     for part in range(levs):
-        high, low = halves(to_modes[part])
+        high, low = halves(to_modes[:, part * levels : (part + 1) * levels])
         to_both[part, :modes_number] = high
         to_both[part, modes_number:] = low
-    high, low = halves(from_modes[...])
-    from_both[0], from_both[1] = high, low
+    for part in range(levs):
+
+        @pl.when(lev == part)
+        def _():
+            high, low = halves(from_modes[part * levels : (part + 1) * levels, :])
+            from_both[0], from_both[1] = high, low
+
     pl.semaphore_wait(barrier, waves + levs - 2)
 
     def packed(slot):
@@ -185,6 +247,7 @@
         size = width_of(c) * LANES
         column = lax.broadcasted_iota(jnp.int32, (1, size), 1) + firsts[c] * LANES
         within = jnp.where(column >= width // 2, column - width // 2, column)
+        column_depth = upright(depth)
 
         @pl.loop(0, pairs)
         def _(pair):
@@ -201,7 +264,7 @@
                 matrix = to_both.at[source]
                 term = product(matrix[...], matrix[:modes_number], block, modes_number)
                 modes = term if modes is None else modes + term
-            scaled = modes / (1.0 + depth[...] * ratio)
+            scaled = modes / (1.0 + column_depth * ratio)
             high, low = halves(scaled)
             from_high = from_both[0]
             result = jnp.dot(from_both[1], high, preferred_element_type=jnp.float32)
@@ -259,18 +322,13 @@
     quad = lax.rem(me, QUAD)
     core = lax.rem(me, 2)
     outer = lax.rem(side + step + 1, 2)
-    cut = levels // 2 // 8 * 8
-    part_rows = levels - cut
-    modes_number = depth.shape[0]
+    part_rows = levels // 2
+    modes_number = depth.shape[1]
     firsts = [sum(parts[:c]) for c in range(chunks)]
     final = chunks - 1
 
     def ring(buffers, c):
-        ref = buffers[c % RING]
-        size = parts[c] * LANES
-        if ref.shape[-1] == size:
-            return ref
-        return ref.at[tuple(slice(None) for _ in ref.shape[:-1]) + (pl.ds(0, size),)]
+        return buffers[c % RING]
 
     def to_wave(index):
         return {"wave": index}
@@ -314,11 +372,16 @@
             barrier, inc=1, device_id={"lev": lax.rem(lev + turn, levs)}, device_id_type=MESH
         )
     for part in range(levs):
-        high, low = halves(to_modes[part])
+        high, low = halves(to_modes[:, part * levels : (part + 1) * levels])
         to_both[part, :modes_number] = high
         to_both[part, modes_number:] = low
-    high, low = halves(from_modes[...])
-    from_both[0], from_both[1] = high, low
+    for part in range(levs):
+
+        @pl.when(lev == part)
+        def _():
+            high, low = halves(from_modes[part * levels : (part + 1) * levels, :])
+            from_both[0], from_both[1] = high, low
+
     pl.semaphore_wait(barrier, waves + levs - 2)
 
     def packed(slot):
@@ -353,27 +416,26 @@
         source = rows_in[c % RING]
         carry, direct = ring(carry_out, c), ring(direct_out, c)
 
-        def pick(slot, target, first, count):
-            for tile in range(parts[c]):
-                target[:, pl.ds(tile * LANES, LANES)] = source[
-                    tile, pl.ds(first * slots + slot, count, stride=slots), :
-                ]
+        def pick(slot, first, count):
+            return source[0, pl.ds(first * slots + slot, count, stride=slots), :]
 
         for mask in range(QUAD - 1, -1, -1):
             carrier = flipped(quad, mask, QUAD)
-            first = lax.rem(carrier, 2) * cut
+            first = lax.rem(carrier, 2) * part_rows
 
             @pl.loop(0, QUAD)
             def _(j):
                 index = (1 - side) * half + lax.div(j, 2) * QUAD
                 index = index + lax.div(carrier, 2) * 2 + lax.rem(j, 2)
-                pick(picks[index], carry.at[mask, j], first, part_rows)
-
-            place = (mask + QUAD * outer) * QUAD
+                carry[mask, pl.ds(j, part_rows, stride=QUAD), :] = pick(
+                    picks[index], first, part_rows
+                )
+
+            place = mask + QUAD * outer
             device = side * half + (1 - side) * QUAD + carrier
 
             def carry_on():
-                target = carried[c].at[pl.ds(place, QUAD)]
+                target = carried[c].at[place]
                 push(carry.at[mask], target, carry_send.at[c], carry_recv.at[c], device)
 
             if mask:
@@ -383,9 +445,7 @@
 
                 @pl.when(outer == 0)
                 def _():
-                    @pl.loop(0, QUAD)
-                    def _(j):
-                        carried[c][j] = carry[0, j]
+                    carried[c][0] = carry[0]
 
         if c == final:
             for mask in range(waves - 1, 0, -1):
@@ -401,7 +461,7 @@
             tail_got[0] = packed(picks[me])
         for mask in range(half - 1, 0, -1):
             index = flipped(me, mask, waves)
-            pick(picks[index], direct.at[mask - 1], 0, levels)
+            direct[mask - 1] = pick(picks[index], 0, levels)
             push(
                 direct.at[mask - 1],
                 received[c].at[mask],
@@ -409,7 +469,7 @@
                 direct_recv.at[c],
                 index,
             )
-        pick(picks[me], received[c].at[0], 0, levels)
+        received[c][0] = pick(picks[me], 0, levels)
         if c + RING < chunks:
             for tile in range(parts[c + RING]):
                 load(c + RING, tile).start()
@@ -417,14 +477,17 @@
     def relay(c):
         @pl.when(outer == 0)
         def _():
-            finish(carried[c].at[pl.ds(QUAD, (half - 1) * QUAD)], carry_recv.at[c])
+            finish(carried[c].at[pl.ds(1, half - 1)], carry_recv.at[c])
             if c >= RING:
                 finish(ring(relay_out, c - RING), relay_send.at[c - RING])
             block = ring(relay_out, c)
 
             @pl.loop(0, room)
             def _(g):
-                block[g] = carried[c][relayed[g]]
+                number = relayed[g]
+                block[pl.ds(g, part_rows, stride=room), :] = carried[c][
+                    lax.div(number, QUAD), pl.ds(lax.rem(number, QUAD), part_rows, stride=QUAD), :
+                ]
 
             push(
                 block, arrived_far[c], relay_send.at[c], relay_recv.at[c],
@@ -442,7 +505,10 @@
 
                 @pl.loop(0, pairs)
                 def _(pair):
-                    block[number, pair] = arrived_far[c][landed[number * pairs + pair]]
+                    start = landed[number * pairs + pair]
+                    block[number, pl.ds(pair, part_rows, stride=pairs), :] = arrived_far[c][
+                        pl.ds(start, part_rows, stride=room), :
+                    ]
 
                 push(
                     block.at[number],
@@ -454,7 +520,10 @@
 
             @pl.loop(0, pairs)
             def _(pair):
-                final_far[c][0, pair] = arrived_far[c][landed[3 * pairs + pair]]
+                start = landed[3 * pairs + pair]
+                final_far[c][0, pl.ds(pair, part_rows, stride=pairs), :] = arrived_far[c][
+                    pl.ds(start, part_rows, stride=room), :
+                ]
 
     def lev_copy(c, turn):
         source, target = (
@@ -500,13 +569,14 @@
         def _(pair):
             place = places[pair]
             far = place >= half
-            near = received[c][lax.rem(place, half)]
-            block[pair, pl.ds(0, cut)] = jnp.where(
-                far, final_far[c][core, pair, pl.ds(0, cut), :], near[:cut]
-            )
-            block[pair, pl.ds(cut, part_rows)] = jnp.where(
-                far, final_far[c][1 - core, pair], near[cut:]
-            )
+            near = lax.rem(place, half)
+            for part, slot in enumerate((core, 1 - core)):
+                first = part * part_rows
+                block[pl.ds(first * pairs + pair, part_rows, stride=pairs), :] = jnp.where(
+                    far,
+                    final_far[c][slot, pl.ds(pair, part_rows, stride=pairs), :],
+                    received[c][near, pl.ds(first, part_rows), :],
+                )
 
         for turn in range(1, levs):
             lev_copy(c, turn).start()
@@ -522,33 +592,45 @@
         size = width_of(c) * LANES
         column = lax.broadcasted_iota(jnp.int32, (1, size), 1) + firsts[c] * LANES
         within = jnp.where(column >= width // 2, column - width // 2, column)
+        column_depth = upright(depth)
         own, results = ring(mine, c), staged[c % RING]
 
-        @pl.loop(0, pairs)
-        def _(pair):
-            wavenumber = me * pairs + pair
-            degree = jnp.where(within <= NT - wavenumber, wavenumber + within, within - 1)
-            ratio = (degree * (degree + 1)).astype(jnp.float32) / float(NT * (NT + 1))
+        @pl.loop(0, pairs // GROUP)
+        def _(number):
+            ratios = []
+            for at in range(GROUP):
+                wavenumber = me * pairs + number * GROUP + at
+                degree = jnp.where(within <= NT - wavenumber, wavenumber + within, within - 1)
+                ratios.append((degree * (degree + 1)).astype(jnp.float32) / float(NT * (NT + 1)))
+            ratio = jnp.concatenate(ratios, axis=1)
             modes = None
             for turn in range(levs):
                 source = lax.rem(lev + levs - turn, levs)
-                block = own[pair] if turn == 0 else theirs[c][turn - 1, pair]
-                if c == final:
-                    tail = tail_mine[pair] if turn == 0 else tail_theirs[turn - 1, pair]
-                    block = jnp.concatenate([block, unpacked(tail)], axis=1)
+                blocks = []
+                for at in range(GROUP):
+                    pair = number * GROUP + at
+                    rows = pl.ds(pair, levels, stride=pairs)
+                    blocks.append(own[rows, :] if turn == 0 else theirs[c][turn - 1, rows, :])
+                    if c == final:
+                        tail = tail_mine[pair] if turn == 0 else tail_theirs[turn - 1, pair]
+                        blocks.append(unpacked(tail))
                 matrix = to_both.at[source]
+                block = jnp.concatenate(blocks, axis=1)
                 term = product(matrix[...], matrix[:modes_number], block, modes_number)
                 modes = term if modes is None else modes + term
-            scaled = modes / (1.0 + depth[...] * ratio)
+            scaled = modes / (1.0 + column_depth * ratio)
             high, low = halves(scaled)
             from_high = from_both[0]
             result = jnp.dot(from_both[1], high, preferred_element_type=jnp.float32)
             result += jnp.dot(from_high, low, preferred_element_type=jnp.float32)
             result += jnp.dot(from_high, high, preferred_element_type=jnp.float32)
-            for tile in range(width_of(c)):
-                results[tile, pl.ds(pair, levels, stride=pairs), :] = result[
-                    :, tile * LANES : (tile + 1) * LANES
-                ]
+            for at in range(GROUP):
+                pair = number * GROUP + at
+                for tile in range(width_of(c)):
+                    first = at * size + tile * LANES
+                    results[tile, pl.ds(pair, levels, stride=pairs), :] = result[
+                        :, first : first + LANES
+                    ]
 
         for tile in range(width_of(c)):
             out_copy(c, tile).start()
@@ -579,11 +661,8 @@
     parts = (1,) * whole
     chunks = len(parts)
     half = waves // 2
-    part_rows = levels - levels // 2 // 8 * 8
+    part_rows = levels // 2
     sizes = (waves, levs, pairs, slots, levels, width, parts, packs, rest, room)
-    widths = [tiles * LANES for tiles in parts]
-    most = [max(parts[c::RING]) for c in range(RING)]
-    ends = [max(parts[c] + (c == chunks - 1) for c in range(k, chunks, RING)) for k in range(RING)]
     vmem, smem, anywhere = (
         pl.BlockSpec(memory_space=space) for space in (pltpu.VMEM, pltpu.SMEM, pl.ANY)
     )
@@ -598,18 +677,18 @@
         out_shape=jax.ShapeDtypeStruct((levels * pairs, (whole + 1) * LANES), f32),
         in_specs=[smem, smem, smem, smem, anywhere, anywhere, vmem, vmem, vmem],
         out_specs=anywhere,
-        scratch_shapes=[vectors(half, levels, size) for size in widths]
-        + [vectors(half * QUAD, part_rows, size) for size in widths]
-        + [vectors(room, part_rows, size) for size in widths]
-        + [vectors(2, pairs, part_rows, size) for size in widths]
-        + [vectors(levs - 1, pairs, levels, size) for size in widths]
-        + [vectors(tiles, levels * slots, LANES) for tiles in most]
-        + [vectors(half - 1, levels, tiles * LANES) for tiles in most]
-        + [vectors(QUAD, QUAD, part_rows, tiles * LANES) for tiles in most]
-        + [vectors(room, part_rows, tiles * LANES) for tiles in most]
-        + [vectors(3, pairs, part_rows, tiles * LANES) for tiles in most]
-        + [vectors(pairs, levels, tiles * LANES) for tiles in most]
-        + [vectors(tiles, levels * pairs, LANES) for tiles in ends]
+        scratch_shapes=[vectors(half, levels, LANES)] * chunks
+        + [vectors(half, QUAD * part_rows, LANES)] * chunks
+        + [vectors(room * part_rows, LANES)] * chunks
+        + [vectors(2, pairs * part_rows, LANES)] * chunks
+        + [vectors(levs - 1, pairs * levels, LANES)] * chunks
+        + [vectors(1, levels * slots, LANES)] * RING
+        + [vectors(half - 1, levels, LANES)] * RING
+        + [vectors(QUAD, QUAD * part_rows, LANES)] * RING
+        + [vectors(room * part_rows, LANES)] * RING
+        + [vectors(3, pairs * part_rows, LANES)] * RING
+        + [vectors(pairs * levels, LANES)] * RING
+        + [vectors(2, levels * pairs, LANES)] * RING
         + [
             vectors(8 * packs * slots, LANES),
             vectors(waves - 1, 8, LANES),
@@ -643,13 +722,7 @@
     groups = owner.shape[0] // waves
     pairs = groups * KPAIR
     modes_number = depth.shape[0]
-    own_index, lev_index = lax.axis_index("wave"), lax.axis_index("lev")
-    numbers = jnp.arange(owner.shape[0], dtype=jnp.int32)
-    mine = owner == own_index
-    before = (numbers[:, None] > numbers[None, :]) & mine[None, :]
-    rank = jnp.sum(before.astype(jnp.int32), axis=1)
-    picks = jnp.sum(jnp.where(mine, rank, 0).reshape(waves, groups), axis=1)
-    places = lax.dynamic_slice_in_dim(owner, own_index * groups, groups) ^ own_index
+    own_index = lax.axis_index("wave")
     whole, rest = width // LANES, width % LANES
     packs = pl.cdiv(levels, 8)
     assert 0 < rest and packs * rest <= LANES
@@ -658,8 +731,6 @@
     sizes = (waves, levs, pairs, slots, levels, width, parts, packs, rest)
     rows = spectral.reshape(levels * slots, width)
     last = jnp.pad(rows[:, whole * LANES :], ((0, 0), (0, LANES - rest)))
-    by_lev = to_modes.reshape(modes_number, levs, levels).transpose(1, 0, 2)
-    own_rows = lax.dynamic_slice_in_dim(from_modes, lev_index * levels, levels)
     vmem, smem, anywhere = (
         pl.BlockSpec(memory_space=space) for space in (pltpu.VMEM, pltpu.SMEM, pl.ANY)
     )
@@ -697,31 +768,31 @@
             collective_id=0, has_side_effects=True, vmem_limit_bytes=67043328
         ),
     )
-    operands = (rows, last, by_lev, own_rows, depth[:, None])
-    if waves == 4 * QUAD:
+    operands = (rows, last, to_modes, from_modes, depth[None, :])
+    if waves == 4 * QUAD and levels % 2 == 0:
         half = waves // 2
         room = half * QUAD * 3 // 4
-        owners = owner.reshape(2, 2, 2, 2, groups).transpose(0, 2, 1, 3, 4).reshape(2, 2, QUAD * groups)
-        crossing = (owners // half != jnp.arange(2)[:, None, None]).astype(jnp.int32)
-        inclusive = jnp.tril(jnp.ones((QUAD * groups,) * 2, jnp.int32))
-        before = jnp.sum(crossing[:, :, None, :] * inclusive, axis=-1)
-        fits = jnp.max(before[:, :, -1]) <= room
-        side, column = own_index // half, own_index // 2 % 2
-        there = before[1 - side, column] - 1
-        taken = (there[None, :] == jnp.arange(room)[:, None]) & (crossing[1 - side, column] > 0)[None, :]
-        target = jnp.arange(QUAD * groups, dtype=jnp.int32) // groups
-        number = ((owners[1 - side, column] ^ own_index) % half) * QUAD + target
-        relayed = jnp.sum(jnp.where(taken, number[None, :], 0), axis=1).astype(jnp.int32)
-        here = jnp.where(crossing[side, column] > 0, before[side, column] - 1, 0).reshape(QUAD, groups)
-        own_target = own_index // QUAD % 2 * 2 + own_index % 2
-        landed = here[own_target ^ jnp.array([3, 2, 1, 0])].reshape(-1).astype(jnp.int32)
+        int_shapes = [waves, groups, room, QUAD * groups, 1]
+        picks, places, relayed, landed, fits = pl.pallas_call(
+            functools.partial(tables, waves, groups, room),
+            out_shape=[jax.ShapeDtypeStruct((size,), jnp.int32) for size in int_shapes],
+            in_specs=[smem],
+            out_specs=[smem] * 5,
+            scratch_shapes=[pltpu.SMEM((4,), jnp.int32)],
+        )(owner)
         solved = lax.cond(
-            fits,
+            fits[0] > 0,
             lambda *given: relay_call(waves, levs, pairs, slots, levels, width, packs, rest, room, whole, modes_number)(*given),
             lambda one, two, three, four, *given: dense(one, two, *given),
             *(picks, places, relayed, landed, *operands),
         )
     else:
+        numbers = jnp.arange(owner.shape[0], dtype=jnp.int32)
+        mine = owner == own_index
+        before = (numbers[:, None] > numbers[None, :]) & mine[None, :]
+        rank = jnp.sum(before.astype(jnp.int32), axis=1)
+        picks = jnp.sum(jnp.where(mine, rank, 0).reshape(waves, groups), axis=1)
+        places = lax.dynamic_slice_in_dim(owner, own_index * groups, groups) ^ own_index
         solved = dense(picks, places, *operands)
     return solved.reshape(levels, pairs, (whole + 1) * LANES)[:, :, :width]
 

time: 255 us -> 227 us (0.89)
  Pallas kernels: 228 us -> 218 us
  local copies, waits for them, and re-layouts: 16.4 us -> 7.53 us
  other arithmetic: 8.38 us -> 0 us
    pallas_call x1, Pallas kernels: 228 us -> 215 us  [per_device(): relay_call(waves, levs, pairs, slots, levels, width, packs, rest, room, w...]
    pallas_call x0 -> x1, Pallas kernels: none -> 2.8 us  [per_device(): pl.pallas_call(functools.partial(tables, waves, groups, room), out_shape=...]
    reshape x6 -> x0, local copies, waits for them, and re-layouts: 2.7 us -> none  [the longest x2 1.19 us: per_device(): by_lev = to_modes.reshape(modes_number, levs, levels).transpose(1, 0, 2)]
    unnamed x7 -> x1, local copies, waits for them, and re-layouts: 6.19 us -> 5.59 us
where the time goes in v3:
time: 227 us; the launch traced here: 226 us
  Pallas kernels  218 us (96%)
  local copies, waits for them, and re-layouts  7.53 us (3%)
    pallas_call x1, Pallas kernels, per_device(): relay_call(waves, levs, pairs, slots, levels, width, packs, rest, room, w...  215 us
    unnamed x1, local copies, waits for them, and re-layouts  5.59 us

profile of v3, /device:TPU:0, one launch (start us, length us, event | category | flops | bytes accessed | tf_op | source)
XLA Modules:
  0.0 226.0 jit_solution(14423516817133292135)
XLA Ops:
  0.0 2.8 %shard_map.57 = (s32[16]{0:T(128)}, s32[8]{0:T(128)}, s32[24]{0:T(128)}, s32[32]{0:T(128)}, s32[1]{0:T(128)}) custom-call(s32[128]{0:T(128)} %owner.1), custom_call_target="tpu_custom_call" | custom-call | tf_op jit(solution)/shard_map/pallas_call | solution.py:776
  3.5 1.1 slice.13
  4.6 0.8 pad.4
  5.4 215.0 %conditional.1 = (f32[68,8,2562]{2,1,0:T(8,128)}) conditional(s32[]{:T(128)} %bitcast.2, (s32[16]{0:T(128)}, s32[8]{0:T(128)}, f32[1088,2562]{1,0:T(8,128)}, f32[1088,128]{1,0:T(8,128)}, f32[136,136]{1,0:T(8,128)}, /*index=5*/f32[136,136]{1,0:T(8,128)}, f32[1,136]{1,0:T(1,128)}) %tuple.21, (s32[16]{0:T(128)}, s32[8]{0:T(128)}, s32[24]{0:T(128)}, ...), branch_computations={%region_0.1_spmd, %region_1.2_spmd} | conditional | bytes 8 | solution.py:783
  5.4 214.8 %branch_1_fun.1 = f32[544,2688]{1,0:T(8,128)} custom-call(s32[16]{0:T(128)} %get-tuple-element.48.picks, s32[8]{0:T(128)} %get-tuple-element.49.places, s32[24]{0:T(128)} %get-tuple-element.50.relayed, s32[32]{0:T(128)} %get-tuple-element.51.landed, f32[1088,2562]{1,0:T(8,128)} %get-tuple-element.52.spectral, f32[1088,128]{1,0:T(8,128)} %get-tuple-element.53.last, ...), custom_call_target="tpu_custom_call" | custom-call | tf_op jit(solution)/shard_map/cond/branch_1_fun/pallas_call | solution.py:785
  220.4 5.6 %copy.11 = f32[68,8,2562]{2,1,0:T(8,128)} copy(f32[68,8,2562]{2,1,0:T(8,128)} %get-tuple-element.67) | data formatting | bytes 11149824

commit v4 on v3

--- a/solution.py
+++ b/solution.py
@@ -17,7 +17,7 @@
 QUAD = 4
 GROUP = 4
 RING = 3
-LAGS = (0, 1, 2, 3, 4)
+LAGS = (0, 1, 1, 2, 3, 4)
 MESH = pl.DeviceIdType.MESH
 
 
@@ -396,8 +396,10 @@
         pieces = [block] + [pltpu.roll(block, LANES - k * rest, 1) for k in range(1, packs)]
         return jnp.concatenate(pieces, axis=0)[:levels]
 
+    def pick(c, slot, first, count):
+        return rows_in[c % RING][0, pl.ds(first * slots + slot, count, stride=slots), :]
+
     def drain_send(c):
-        finish(ring(direct_out, c), direct_send.at[c])
         carry = ring(carry_out, c)
 
         @pl.when(outer == 1)
@@ -413,11 +415,7 @@
             load(c, tile).wait()
         if c >= RING:
             drain_send(c - RING)
-        source = rows_in[c % RING]
-        carry, direct = ring(carry_out, c), ring(direct_out, c)
-
-        def pick(slot, first, count):
-            return source[0, pl.ds(first * slots + slot, count, stride=slots), :]
+        carry = ring(carry_out, c)
 
         for mask in range(QUAD - 1, -1, -1):
             carrier = flipped(quad, mask, QUAD)
@@ -428,7 +426,7 @@
                 index = (1 - side) * half + lax.div(j, 2) * QUAD
                 index = index + lax.div(carrier, 2) * 2 + lax.rem(j, 2)
                 carry[mask, pl.ds(j, part_rows, stride=QUAD), :] = pick(
-                    picks[index], first, part_rows
+                    c, picks[index], first, part_rows
                 )
 
             place = mask + QUAD * outer
@@ -447,6 +445,10 @@
                 def _():
                     carried[c][0] = carry[0]
 
+    def near(c):
+        if c >= RING:
+            finish(ring(direct_out, c - RING), direct_send.at[c - RING])
+        direct = ring(direct_out, c)
         if c == final:
             for mask in range(waves - 1, 0, -1):
                 index = flipped(me, mask, waves)
@@ -461,7 +463,7 @@
             tail_got[0] = packed(picks[me])
         for mask in range(half - 1, 0, -1):
             index = flipped(me, mask, waves)
-            direct[mask - 1] = pick(picks[index], 0, levels)
+            direct[mask - 1] = pick(c, picks[index], 0, levels)
             push(
                 direct.at[mask - 1],
                 received[c].at[mask],
@@ -469,7 +471,7 @@
                 direct_recv.at[c],
                 index,
             )
-        received[c][0] = pick(picks[me], 0, levels)
+        received[c][0] = pick(c, picks[me], 0, levels)
         if c + RING < chunks:
             for tile in range(parts[c + RING]):
                 load(c + RING, tile).start()
@@ -635,7 +637,7 @@
         for tile in range(width_of(c)):
             out_copy(c, tile).start()
 
-    stages = (send, relay, forward, gather, solve)
+    stages = (send, relay, near, forward, gather, solve)
     for turn in range(chunks + LAGS[-1]):
         for stage, lag in zip(stages, LAGS):
             if 0 <= turn - lag < chunks:
@@ -645,6 +647,7 @@
         lev_copy(chunks, turn).wait_send()
     for c in range(max(chunks - RING, 0), chunks):
         drain_send(c)
+        finish(ring(direct_out, c), direct_send.at[c])
 
         @pl.when(outer == 0)
         def _():

time: 227 us -> 226 us (level)
  no operation moved by 1% of the time
where the time goes in v4:
time: 226 us; the launch traced here: 225 us
  Pallas kernels  216 us (96%)
  local copies, waits for them, and re-layouts  7.53 us (3%)
    pallas_call x1, Pallas kernels, per_device(): relay_call(waves, levs, pairs, slots, levels, width, packs, rest, room, w...  214 us
    unnamed x1, local copies, waits for them, and re-layouts  5.59 us

profile of v4, /device:TPU:0, one launch (start us, length us, event | category | flops | bytes accessed | tf_op | source)
XLA Modules:
  0.0 225.0 jit_solution(16688102644199822097)
XLA Ops:
  0.0 2.8 %shard_map.57 = (s32[16]{0:T(128)}, s32[8]{0:T(128)}, s32[24]{0:T(128)}, s32[32]{0:T(128)}, s32[1]{0:T(128)}) custom-call(s32[128]{0:T(128)} %owner.1), custom_call_target="tpu_custom_call" | custom-call | tf_op jit(solution)/shard_map/pallas_call | solution.py:779
  3.5 1.1 slice.13
  4.6 0.8 pad.4
  5.4 214.0 %conditional.1 = (f32[68,8,2562]{2,1,0:T(8,128)}) conditional(s32[]{:T(128)} %bitcast.2, (s32[16]{0:T(128)}, s32[8]{0:T(128)}, f32[1088,2562]{1,0:T(8,128)}, f32[1088,128]{1,0:T(8,128)}, f32[136,136]{1,0:T(8,128)}, /*index=5*/f32[136,136]{1,0:T(8,128)}, f32[1,136]{1,0:T(1,128)}) %tuple.21, (s32[16]{0:T(128)}, s32[8]{0:T(128)}, s32[24]{0:T(128)}, ...), branch_computations={%region_0.1_spmd, %region_1.2_spmd} | conditional | bytes 8 | solution.py:786
  5.4 213.7 %branch_1_fun.1 = f32[544,2688]{1,0:T(8,128)} custom-call(s32[16]{0:T(128)} %get-tuple-element.48.picks, s32[8]{0:T(128)} %get-tuple-element.49.places, s32[24]{0:T(128)} %get-tuple-element.50.relayed, s32[32]{0:T(128)} %get-tuple-element.51.landed, f32[1088,2562]{1,0:T(8,128)} %get-tuple-element.52.spectral, f32[1088,128]{1,0:T(8,128)} %get-tuple-element.53.last, ...), custom_call_target="tpu_custom_call" | custom-call | tf_op jit(solution)/shard_map/cond/branch_1_fun/pallas_call | solution.py:788
  219.4 5.6 %copy.11 = f32[68,8,2562]{2,1,0:T(8,128)} copy(f32[68,8,2562]{2,1,0:T(8,128)} %get-tuple-element.67) | data formatting | bytes 11149824
